TPU v7x, 32 devices: a whole 2x2x4 slice. The times are simulated.
32 devices in a mesh: rep: 4 (over y, x), wide: 8 (over z, core).
Axes of the slice: x: 2, y: 2, z: 4, core: 2. Of those that a mesh axis runs over, the one named last changes fastest.
Arguments:
- hot_table: bfloat16 [16384, 128], P('wide'), may hold values from -3 to 3
- cold_table: bfloat16 [65536, 128], P(('rep', 'wide')), may hold values from -3 to 3
- bag_of: int32 [32, 6144], P(('rep', 'wide')), may hold values from 0 to 4095, never falling along the last dimension, each value on 1 to 4 neighbouring positions
- owner: int32 [196608, 1], P(('rep', 'wide')), may hold values from 0 to 39; in each aligned block of 6144 rows (0 to 6143, 6144 to 12287, ...) at most 232 rows name the same one
- row_in: int32 [196608], P(('rep', 'wide')), may hold values from 0 to 2047
- cross_down: bfloat16 [4096, 256], replicated, may hold values from -0.09375 to 0.09375
- cross_up: bfloat16 [4096, 256], replicated, may hold values from -0.375 to 0.375
- cross_bias: float32 [4096], replicated, may hold values from -3 to 3
- top_weight: bfloat16 [4096, 512], replicated, may hold values from -0.09375 to 0.09375
- d_hidden: bfloat16 [4096, 512], P(('rep', 'wide')), may hold values from -6 to 6
Outputs:
- grad_up: float32 [4096, 256], P(('rep', 'wide'))
- grad_down: float32 [4096, 256], P(('rep', 'wide'))
- grad_top: float32 [4096, 512], P(('rep', 'wide'))
- hot_grad: float32 [16384, 128], P('wide')
- cold_grad: float32 [65536, 128], P(('rep', 'wide'))
Inputs may be any that keep to these rules, and one draw needn't show every extreme that they name: Destination of each lookup: below 8 the holder of hot rows at that wide index in the asking device's own rep group, else the holder of cold rows numbered owner minus 8 over rep+wide. Among the 6144 lookups of one device no destination is named more than 232 times, and in every draw some device names some destination exactly 232 times. `bag_of`: never falls along one device's lookups; each of a device's 4096 bags has 1 to 4 lookups, and some bag has 4. Bag b is sample b // 32, feature b % 32 of the device.
All inputs are finite; a program needn't handle non-finite values.
Results may differ from a plain program's by a relative error of at most 0.0064.
Values may be sent and summed in bfloat16 or wider, within the bound.
No kernel may reach another device: no remote copies, remote signals or barrier semaphores. Data moves between devices by JAX's collectives and lax.ppermute only.
A program may use at most 128 MiB of HBM per device.

v0:
```python
import math

import jax
import jax.numpy as jnp
from jax import lax
from jax.sharding import PartitionSpec as P


def blocked(total, values, fn):
    block = math.gcd(total, 512)
    index_blocks = jnp.arange(total, dtype=jnp.int32).reshape(total // block, block)
    if values is None:
        result = lax.map(fn, index_blocks)
    else:
        result = lax.map(
            lambda pair: fn(pair[0], pair[1]), (index_blocks, values.reshape(total // block, block))
        )
    return jax.tree.map(lambda part: part.reshape((total,) + part.shape[2:]), result)


def accumulate(incoming, asked, rows_dev, width):
    capacity = asked.shape[-1]
    sources = asked.size // capacity
    group = 1
    for cand in range(1, sources + 1):
        if sources % cand == 0 and cand * capacity <= 2048:
            group = cand
    steps_count = sources // group
    inc_blocks = incoming.reshape(steps_count, group * capacity, width)
    ask_blocks = asked.reshape(steps_count, group * capacity)
    row_ids = jnp.arange(rows_dev, dtype=jnp.int32)

    def add_block(total, pair):
        inc_block, ask_block = pair
        selector = (row_ids[:, None] == ask_block[None, :]).astype(jnp.bfloat16)
        return (total + jnp.dot(selector, inc_block, preferred_element_type=jnp.float32), None)

    summed, unused = lax.scan(
        add_block, jnp.zeros((rows_dev, width), jnp.float32), (inc_blocks, ask_blocks)
    )
    return summed


def body(
    hot_table,
    cold_table,
    bag_of,
    owner,
    row_in,
    cross_down,
    cross_up,
    cross_bias,
    top_weight,
    d_hidden,
):
    n_rep = lax.axis_size("rep")
    n_wide = lax.axis_size("wide")
    shards = n_rep * n_wide
    dests = n_wide + shards
    look_dev = row_in.shape[0]
    rows_dev = hot_table.shape[0]
    width = hot_table.shape[1]
    batch_dev = d_hidden.shape[0]
    feat_width = cross_down.shape[0]
    rank_width = cross_down.shape[1]
    features = feat_width // width
    bags_dev = batch_dev * features
    capacity = max(8, (3 * look_dev // (2 * dests) + 7) // 8 * 8)
    bag_list = bag_of[0]
    dest_list = owner[:, 0]
    positions = jnp.arange(look_dev, dtype=jnp.int32)

    def rank_block(ids, dest_block):
        earlier = (dest_list[None, :] == dest_block[:, None]) & (positions[None, :] < ids[:, None])
        return jnp.sum(earlier.astype(jnp.int32), axis=1)

    ranks = blocked(look_dev, dest_list, rank_block)
    slots = dest_list * capacity + ranks
    slot_total = dests * capacity

    def slot_info_block(ids):
        match = slots[None, :] == ids[:, None]
        used = jnp.sum(match.astype(jnp.int32), axis=1)
        row_pick = jnp.sum(jnp.where(match, row_in[None, :], 0), axis=1)
        bag_pick = jnp.sum(jnp.where(match, bag_list[None, :], 0), axis=1)
        return (used, row_pick, bag_pick)

    used_count, row_pick, bag_pick = blocked(slot_total, None, slot_info_block)
    filled = used_count > 0
    request = jnp.where(filled, row_pick, rows_dev)
    hot_request = request[: n_wide * capacity].reshape(n_wide, capacity)
    cold_request = request[n_wide * capacity :]
    pieces = lax.all_to_all(hot_request, "wide", split_axis=0, concat_axis=0, tiled=True)
    found = jnp.take(hot_table, pieces, axis=0, mode="fill", fill_value=0)
    hot_back = lax.all_to_all(found, "wide", split_axis=0, concat_axis=0, tiled=True)
    hot_asked = pieces
    pieces = lax.all_to_all(
        cold_request.reshape(shards, capacity),
        ("rep", "wide"),
        split_axis=0,
        concat_axis=0,
        tiled=True,
    )
    found = jnp.take(cold_table, pieces, axis=0, mode="fill", fill_value=0)
    cold_back = lax.all_to_all(found, ("rep", "wide"), split_axis=0, concat_axis=0, tiled=True)
    returned = jnp.concatenate([hot_back.reshape(-1, width), cold_back.reshape(-1, width)], axis=0)
    look_rows = returned[slots]
    bag_block = math.gcd(bags_dev, 512)
    bag_starts = jnp.arange(bags_dev // bag_block, dtype=jnp.int32) * bag_block
    bag_offsets = jnp.arange(bag_block, dtype=jnp.int32)

    def pool_block(first):
        selector = ((first + bag_offsets)[:, None] == bag_list[None, :]).astype(jnp.bfloat16)
        return jnp.dot(selector, look_rows, preferred_element_type=jnp.float32)

    pooled = lax.map(pool_block, bag_starts)
    base = pooled.reshape(batch_dev, feat_width).astype(jnp.bfloat16)
    low = jnp.dot(base, cross_down, preferred_element_type=jnp.float32).astype(jnp.bfloat16)
    cross = (
        lax.dot_general(low, cross_up, (((1,), (1,)), ((), ())), preferred_element_type=jnp.float32)
        + cross_bias
    )
    base_full = base.astype(jnp.float32)
    mixed = (base_full * cross + base_full).astype(jnp.bfloat16)
    preact = jnp.dot(mixed, top_weight, preferred_element_type=jnp.float32)
    sigm = jax.nn.sigmoid(preact)
    d_pre = (d_hidden.astype(jnp.float32) * sigm * (1.0 + preact * (1.0 - sigm))).astype(
        jnp.bfloat16
    )
    d_mixed = lax.dot_general(
        d_pre, top_weight, (((1,), (1,)), ((), ())), preferred_element_type=jnp.float32
    )
    d_cross = (d_mixed * base_full).astype(jnp.bfloat16)
    d_low = jnp.dot(d_cross, cross_up, preferred_element_type=jnp.float32).astype(jnp.bfloat16)
    d_base = (
        d_mixed * (cross + 1.0)
        + lax.dot_general(
            d_low, cross_down, (((1,), (1,)), ((), ())), preferred_element_type=jnp.float32
        )
    ).astype(jnp.bfloat16)
    scale_factor = 1.0 / math.sqrt(batch_dev * shards)
    contract = (((0,), (0,)), ((), ()))
    t_up = lax.dot_general(d_cross, low, contract, preferred_element_type=jnp.float32)
    t_down = lax.dot_general(base, d_low, contract, preferred_element_type=jnp.float32)
    t_top = lax.dot_general(mixed, d_pre, contract, preferred_element_type=jnp.float32)
    summed = lax.psum_scatter(
        jnp.concatenate([t_up, t_down, t_top], axis=1) * scale_factor,
        ("rep", "wide"),
        scatter_dimension=0,
        tiled=True,
    )
    bag_rows = d_base.reshape(bags_dev, width)
    outgoing = jnp.where(filled[:, None], bag_rows[bag_pick], jnp.zeros((), jnp.bfloat16))
    hot_in = lax.all_to_all(
        outgoing[: n_wide * capacity].reshape(n_wide, capacity, width),
        "wide",
        split_axis=0,
        concat_axis=0,
        tiled=True,
    )
    cold_part = outgoing[n_wide * capacity :]
    cold_in = lax.all_to_all(
        cold_part.reshape(shards, capacity, width),
        ("rep", "wide"),
        split_axis=0,
        concat_axis=0,
        tiled=True,
    )
    hot_grad = lax.psum(accumulate(hot_in, hot_asked, rows_dev, width), "rep")
    cold_grad = accumulate(cold_in, pieces, rows_dev, width)
    return (
        summed[:, :rank_width],
        summed[:, rank_width : 2 * rank_width],
        summed[:, 2 * rank_width :],
        hot_grad,
        cold_grad,
    )


def solution(mesh):
    placed = (
        P("wide", None),
        P(("rep", "wide"), None),
        P(("rep", "wide"), None),
        P(("rep", "wide"), None),
        P(("rep", "wide")),
        P(),
        P(),
        P(),
        P(),
        P(("rep", "wide"), None),
    )
    return jax.shard_map(
        body,
        mesh=mesh,
        in_specs=placed,
        out_specs=(
            P(("rep", "wide"), None),
            P(("rep", "wide"), None),
            P(("rep", "wide"), None),
            P("wide", None),
            P(("rep", "wide"), None),
        ),
        check_vma=False,
    )
```

profile of v0, /device:TPU:0, one launch (start us, length us, event | category | flops | bytes accessed | tf_op | source)
XLA Modules:
  0.0 695.0 jit_solution(16218551975108877859)
XLA Ops:
  10.1 42.3 %while.56 = (s32[]{:T(128)}, s32[12,512]{1,0:T(8,128)S(1)}, s32[6144,1]{0,1:T(1,128)}, s32[12,512]{1,0:T(8,128)S(1)}, s32[12,512]{1,0:T(8,128)S(1)}) while((s32[]{:T(128)}, s32[12,512]{1,0:T(8,128)S(1)}, s32[6144,1]{0,1:T(1,128)}, s32[12,512]{1,0:T(8,128)S(1)}, s32[12,512]{1,0:T(8,128)S(1)}) %tuple.101), condition=%wide.region_2.3_spmd.clone.clone, body=%wide.region_0.2_spmd.clone.sunk.clone | while | flops 15728130 | bytes 43085 | solution.py:15
  10.1 3.4 convert_reduce_fusion.3
  13.6 3.4 convert_reduce_fusion.3
  17.1 3.4 convert_reduce_fusion.3
  20.7 3.4 convert_reduce_fusion.3
  24.2 3.4 convert_reduce_fusion.3
  27.7 3.4 convert_reduce_fusion.3
  31.2 3.4 convert_reduce_fusion.3
  34.8 3.4 convert_reduce_fusion.3
  38.3 3.4 convert_reduce_fusion.3
  41.8 3.4 convert_reduce_fusion.3
  45.3 3.4 convert_reduce_fusion.3
  48.9 3.4 convert_reduce_fusion.3
  53.2 212.2 %while.55 = (s32[]{:T(128)}, s32[145,64]{1,0:T(8,128)S(1)}, s32[145,64]{1,0:T(8,128)S(1)}, s32[145,64]{1,0:T(8,128)S(1)}, s32[6144]{0:T(1024)S(1)}, /*index=5*/s...) while((s32[]{:T(128)}, s32[145,64]{1,0:T(8,128)S(1)}, s32[145,64]{1,0:T(8,128)S(1)}, ...), condition=%wide.region_7.8_spmd.clone, body=%wide.region_3.7_spmd.sunk.clone | while | flops 2752322 | bytes 76909 | solution.py:13
  266.1 6.4 all-to-all-start
  273.2 4.8 all-to-all-done
  281.1 4.3 gather_fusion
  288.2 3.5 all-to-all-start.1
  291.9 15.8 %gather_fusion.1 = bf16[7424,128]{1,0:T(8,128)(2,1)} fusion(bf16[2048,128]{1,0:T(8,128)(2,1)S(1)} %copy-done.2, s32[8192]{0:T(1024)S(1)} %pad_clamp_fusion.1), kind=kCustom, calls=%fused_computation.1 | custom fusion | bytes 3830784 | tf_op jit(solution)/shard_map/jit(_take)/gather | solution.py:104
  307.7 4.3 broadcast_select_fusion.1
  312.0 5.8 all-to-all-start.3
  318.1 45.5 %all-to-all-done.3 = bf16[32,232,128]{2,1,0:T(8,128)(2,1)} async-done(((bf16[32,232,128]{2,1,0:T(8,128)(2,1)}), bf16[32,232,128]{2,1,0:T(8,128)(2,1)}, u32[]{:S(2)}, u32[]{:S(2)}) %all-to-all-start.3) | async-done | bytes 1900576 | tf_op jit(solution)/shard_map/all_to_all | solution.py:105
  363.6 4.0 pad_maximum_fusion
  367.6 23.1 %gather_fusion.2 = bf16[6144,128]{1,0:T(8,128)(2,1)} fusion(bf16[9280,128]{1,0:T(8,128)(2,1)} %pad_maximum_fusion, s32[6144]{0:T(1024)S(1)} %broadcast_clamp_fusion), kind=kCustom, calls=%fused_computation.2 | custom fusion | bytes 3170304 | tf_op jit(solution)/shard_map/gather | solution.py:107
  390.7 41.2 %while.57 = (s32[]{:T(128)}, bf16[8,512,128]{2,1,0:T(8,128)(2,1)}, s32[8]{0:T(128)S(1)}, s32[1,6144]{1,0:T(1,128)S(1)}, bf16[6144,128]{1,0:T(8,128)(2,1)}) while((s32[]{:T(128)}, bf16[8,512,128]{2,1,0:T(8,128)(2,1)}, s32[8]{0:T(128)S(1)}, s32[1,6144]{1,0:T(1,128)S(1)}, bf16[6144,128]{1,0:T(8,128)(2,1)}) %tuple.119), condition=%wide.region_9.10_spmd.clone.clone, body=%wide.region_8.9_spmd.clone.sunk.clone | while | flops 808452608 | bytes 1863769 | solution.py:116
  391.9 3.9 fusion.79
  397.1 3.9 fusion.79
  402.2 3.9 fusion.79
  407.4 3.9 fusion.79
  412.5 3.9 fusion.79
  417.7 3.9 fusion.79
  422.8 3.9 fusion.79
  428.0 3.9 fusion.79
  444.4 6.3 maximum_multiply_fusion
  452.3 3.1 fusion.28
  455.9 19.8 %gather_fusion.3 = bf16[9280,128]{1,0:T(8,128)(2,1)} fusion(bf16[4096,128]{1,0:T(8,128)(2,1)S(1)} %reshape.214, s32[10240]{0:T(1024)S(1)} %pad_clamp_fusion), kind=kCustom, calls=%fused_computation.3 | custom fusion | bytes 4788480 | tf_op jit(solution)/shard_map/gather | solution.py:153
  475.8 6.7 broadcast_select_fusion
  484.7 3.5 all-to-all-start.4
  488.2 2.9 slice.46
  491.1 19.3 %all-to-all-done.4 = bf16[8,232,128]{2,1,0:T(8,128)(2,1)S(1)} async-done(((bf16[8,232,128]{2,1,0:T(8,128)(2,1)}), bf16[8,232,128]{2,1,0:T(8,128)(2,1)S(1)}, u32[]{:S(2)}, u32[]{:S(2)}) %all-to-all-start.4) | async-done | bytes 475168 | tf_op jit(solution)/shard_map/all_to_all | solution.py:154
  513.7 3.8 fusion.26
  517.5 68.6 %all-to-all-done.5 = bf16[32,232,128]{2,1,0:T(8,128)(2,1)S(1)} async-done(((bf16[32,232,128]{2,1,0:T(8,128)(2,1)}), bf16[32,232,128]{2,1,0:T(8,128)(2,1)S(1)}, u32[]{:S(2)}, u32[]{:S(2)}) %all-to-all-start.5) | async-done | bytes 1900576 | tf_op jit(solution)/shard_map/all_to_all | solution.py:162
  586.1 19.2 %while.58 = (s32[]{:T(128)}, f32[2048,128]{1,0:T(8,128)}, s32[4,1856]{1,0:T(4,128)S(1)}, bf16[4,1856,128]{2,1,0:T(8,128)(2,1)S(1)}) while((s32[]{:T(128)}, f32[2048,128]{1,0:T(8,128)}, s32[4,1856]{1,0:T(4,128)S(1)}, bf16[4,1856,128]{2,1,0:T(8,128)(2,1)S(1)}) %tuple.118), condition=%wide.region_13.14_spmd.clone.clone, body=%wide.region_12.13_spmd.clone.sunk.clone | while | flops 977403904 | bytes 2595407 | solution.py:38
  586.1 3.8 fusion.81
  590.0 5.1 fusion.81
  595.0 5.1 fusion.81
  600.1 5.1 fusion.81
  605.2 75.8 %reduce-scatter.2.cloned.1.call-done = f32[128,1024]{0,1:T(8,128)} async-done(((f32[4096,1024]{0,1:T(8,128)}), f32[128,1024]{0,1:T(8,128)}) %reduce-scatter.2.cloned.1.call-update) | async-done | bytes 524304 | tf_op jit(solution)/shard_map/reduce_scatter | solution.py:146
  (858 shorter events, 256.8 us)
Async XLA Ops:
  8.0 427.5 %copy-start = (bf16[4096,256]{1,0:T(8,128)(2,1)S(1)}, bf16[4096,256]{1,0:T(8,128)(2,1)}, u32[]{:S(2)}) copy-start(bf16[4096,256]{1,0:T(8,128)(2,1)} %param.24) | copy-start | bytes 6291460
  8.0 273.0 %copy-start.6 = (bf16[2048,128]{1,0:T(8,128)(2,1)S(1)}, bf16[2048,128]{1,0:T(8,128)(2,1)}, u32[]{:S(2)}) copy-start(bf16[2048,128]{1,0:T(8,128)(2,1)} %param.18) | copy-start | bytes 1572868
  266.1 12.0 %all-to-all-start = ((s32[8,1,232]{2,1,0:T(1,128)}), s32[8,1,232]{2,1,0:T(1,128)S(1)}, u32[]{:S(2)}, u32[]{:S(2)}) async-start(s32[8,1,232]{2,1,0:T(1,128)} %all_to_all.32), calls=%async_computation | async-start | bytes 16384 | tf_op jit(solution)/shard_map/all_to_all | solution.py:93
  278.1 10.1 %all-to-all-start.2 = ((s32[32,1,232]{2,1,0:T(1,128)}), s32[32,1,232]{2,1,0:T(1,128)S(1)}, u32[]{:S(2)}, u32[]{:S(2)}) async-start(s32[32,1,232]{2,1,0:T(1,128)} %all_to_all.44), calls=%async_computation.2 | async-start | bytes 65536 | tf_op jit(solution)/shard_map/all_to_all | solution.py:97
  285.3 6.6 copy-start.2
  288.2 23.8 %all-to-all-start.1 = ((bf16[8,232,128]{2,1,0:T(8,128)(2,1)}), bf16[8,232,128]{2,1,0:T(8,128)(2,1)S(1)}, u32[]{:S(2)}, u32[]{:S(2)}) async-start(bf16[8,232,128]{2,1,0:T(8,128)(2,1)} %broadcast_select_fusion.2), calls=%async_computation.1 | async-start | bytes 950272 | tf_op jit(solution)/shard_map/all_to_all | solution.py:95
  312.0 51.6 %all-to-all-start.3 = ((bf16[32,232,128]{2,1,0:T(8,128)(2,1)}), bf16[32,232,128]{2,1,0:T(8,128)(2,1)}, u32[]{:S(2)}, u32[]{:S(2)}) async-start(bf16[32,232,128]{2,1,0:T(8,128)(2,1)} %broadcast_select_fusion.1), calls=%async_computation.3 | async-start | bytes 3801088 | tf_op jit(solution)/shard_map/all_to_all | solution.py:105
  317.8 363.2 %reduce-scatter.2.cloned.1.call-start = ((), (), s32[]{:S(2)}) async-start(), calls=%async_computation.7 | async-start | bytes 17301504 | tf_op jit(solution)/shard_map/reduce_scatter | solution.py:146
  367.6 23.1 %copy-start.9 = (s32[1,6144]{1,0:T(1,128)S(1)}, s32[1,6144]{1,0:T(1,128)}, u32[]{:S(2)}) copy-start(s32[1,6144]{1,0:T(1,128)} %get-tuple-element.565) | copy-start | bytes 73732
  433.4 2.1 copy-start.11
  435.5 2.2 copy-start.7
  437.7 4.7 copy-start.3
  437.7 1.0 copy-start.10
  440.2 1.3 copy-start.5
  450.7 1.6 copy-start.4
  482.5 1.4 copy-start.8
  484.7 25.7 %all-to-all-start.4 = ((bf16[8,232,128]{2,1,0:T(8,128)(2,1)}), bf16[8,232,128]{2,1,0:T(8,128)(2,1)S(1)}, u32[]{:S(2)}, u32[]{:S(2)}) async-start(bf16[8,232,128]{2,1,0:T(8,128)(2,1)} %bitcast.13), calls=%async_computation.5 | async-start | bytes 950272 | tf_op jit(solution)/shard_map/all_to_all | solution.py:154
  510.4 75.7 %all-to-all-start.5 = ((bf16[32,232,128]{2,1,0:T(8,128)(2,1)}), bf16[32,232,128]{2,1,0:T(8,128)(2,1)S(1)}, u32[]{:S(2)}, u32[]{:S(2)}) async-start(bf16[32,232,128]{2,1,0:T(8,128)(2,1)} %bitcast.15), calls=%async_computation.6 | async-start | bytes 3801088 | tf_op jit(solution)/shard_map/all_to_all | solution.py:162
  513.1 172.2 %all-reduce.2.cloned.1.call-start = ((), (), s32[]{:S(2)}) async-start(), calls=%async_computation.8 | async-start | bytes 2097152 | tf_op jit(solution)/shard_map/psum | solution.py:169
  605.2 82.3 %copy-start.1 = (bf16[4096,256]{1,0:T(8,128)(2,1)S(1)}, bf16[4096,256]{1,0:T(8,128)(2,1)}, u32[]{:S(2)}) copy-start(bf16[4096,256]{1,0:T(8,128)(2,1)} %param.24) | copy-start | bytes 6291460
Sparse Core Ops, SparseCore 0:
  450.9 230.0 reduce-scatter.1
Sparse Core Ops, SparseCore 1:
  517.6 70.8 all-reduce.1
where the time goes:
time: 709 us; the launch traced here: 695 us
  other arithmetic  262 us (37%)
  waiting for transfers between devices  216 us (30%)
  local copies, waits for them, and re-layouts  106 us (15%)
  matrix products  65.7 us (9%)
  starting transfers between devices  25.2 us (4%)
  between operations  16 us (2%)
    reduce_sum x145, other arithmetic, slot_info_block(): bag_pick = jnp.sum(jnp.where(match, bag_list[None, :], 0), axis=1)  191 us
    reduce_scatter x1, waiting for transfers between devices, body(): lax.psum_scatter(jnp.concatenate([t_up, t_down, t_top], axis=1) * scale_f...  75.8 us
    all_to_all x1, waiting for transfers between devices, body(): lax.all_to_all(cold_part.reshape(shards, capacity, width), ('rep', 'wide'...  68.6 us
    all_to_all x1, waiting for transfers between devices, body(): lax.all_to_all(found, ('rep', 'wide'), split_axis=0, concat_axis=0, tiled...  45.5 us
    reduce_sum x12, other arithmetic, rank_block(): return jnp.sum(earlier.astype(jnp.int32), axis=1)  41.1 us
    dot_general x8, matrix products, pool_block(): return jnp.dot(selector, look_rows, preferred_element_type=jnp.float32)  31.3 us
    gather x1, local copies, waits for them, and re-layouts, body(): look_rows = returned[slots]  23.1 us
    dot_general x5, matrix products, add_block(): jnp.dot(selector, inc_block, preferred_element_type=jnp.float32)  22.8 us
  transfers between devices with their start and end apart: 8, of which 6 were waited for; matrix products, arithmetic and copies ran while one was open for 13% of the time, Pallas kernels for 0%

commit v1 on v0

v1 whole, which is shorter than its diff:
```python
import functools
import math

import jax
import jax.numpy as jnp
from jax import lax
from jax.experimental import pallas as pl
from jax.experimental.pallas import tpu as pltpu
from jax.sharding import Mesh
from jax.sharding import PartitionSpec as P

LANES = 128
CORES = 2
BF = jnp.bfloat16
F32 = jnp.float32
NT = (((1,), (1,)), ((), ()))


def round_up(value, unit):
    return (value + unit - 1) // unit * unit


def route_kernel(
    owner_ref, row_ref, bag_ref, slots_ref, rows_ref, bags_ref, carry, acc, *, n_rep, n_wide, cap, per_dest, hot_at
):
    blocks = owner_ref.shape[0]
    dests = carry.shape[0]
    shards, lanes = rows_ref.shape
    owner_ids = lax.broadcasted_iota(jnp.int32, (dests, LANES), 0)
    dest_ids = lax.broadcasted_iota(jnp.int32, (shards, LANES), 0)
    place_ids = lax.broadcasted_iota(jnp.int32, (lanes, LANES), 0)
    before = lax.broadcasted_iota(jnp.int32, (LANES, 2 * LANES), 0)
    after = lax.broadcasted_iota(jnp.int32, (LANES, 2 * LANES), 1)
    upper = jnp.where((before < after), 1.0, 0.0).astype(BF)
    carry[...] = jnp.zeros_like(carry)
    acc[...] = jnp.zeros_like(acc)

    def step(block, unused):
        own = owner_ref[pl.ds(block, 1), :]
        mine = owner_ids == own
        counts = jnp.dot(jnp.where(mine, 1.0, 0.0).astype(BF), upper, preferred_element_type=F32)
        earlier = counts[:, :LANES] + carry[...]
        carry[...] += counts[:, LANES:]
        rank = jnp.sum(jnp.where(mine, earlier, 0.0), axis=0, keepdims=True)
        layer = jnp.floor((rank + 0.5) * (1.0 / n_rep))
        copy_at = (rank - layer * n_rep).astype(jnp.int32)
        layer = layer.astype(jnp.int32)
        rank = rank.astype(jnp.int32)
        is_hot = own < n_wide
        dest = jnp.where(is_hot, copy_at * n_wide + own, own - n_wide)
        place = jnp.where(is_hot, hot_at + layer, rank)
        slots_ref[pl.ds(block, 1), :] = dest * per_dest + jnp.where(is_hot, cap + layer, rank)
        at_dest = dest_ids == dest
        at_place = jnp.where(place_ids == place, 1.0, 0.0).astype(BF)
        row = row_ref[pl.ds(block, 1), :] + 1
        bag = bag_ref[pl.ds(block, 1), :]
        planes = [row // 256, row % 256, bag // 256, bag % 256]
        left = jnp.concatenate([jnp.where(at_dest, plane.astype(F32), 0.0) for plane in planes], axis=0)
        acc[...] += lax.dot_general(left.astype(BF), at_place, NT, preferred_element_type=F32)
        return unused

    lax.fori_loop(0, blocks, step, 0)
    rows_ref[...] = (acc[:shards] * 256.0 + acc[shards : 2 * shards]).astype(jnp.int32)
    bags_ref[...] = (acc[2 * shards : 3 * shards] * 256.0 + acc[3 * shards :]).astype(jnp.int32)


def narrow(source, target):
    total = target.shape[0]
    step = math.gcd(total, 512)

    def move(at, unused):
        rows = pl.ds(pl.multiple_of(at * step, step), step)
        target[rows, :] = source[rows, :].astype(target.dtype)
        return unused

    lax.fori_loop(0, total // step, move, 0)


def widen(source, target):
    total = source.shape[0]
    step = math.gcd(total, 512)

    def move(at, unused):
        rows = pl.ds(pl.multiple_of(at * step, step), step)
        target[rows, :] = source[rows, :].astype(F32)
        return unused

    lax.fori_loop(0, total // step, move, 0)


def serve_kernel(ask_ref, cold_ref, hot_ref, out_ref, cold, hot, stage, *, cap, hot_cap, hot_at):
    shards = ask_ref.shape[0]
    per_dest = cap + hot_cap
    cold[0:8, :] = jnp.zeros((8, LANES), F32)
    hot[0:8, :] = jnp.zeros((8, LANES), F32)
    rows = cold_ref.shape[0]
    cold[8 : 8 + rows, :] = cold_ref[...].astype(F32)
    hot[8 : 8 + rows, :] = hot_ref[...].astype(F32)

    def step(source, unused):
        first = pl.multiple_of(source * per_dest, 8)
        for at in range(cap):
            stage[pl.ds(first + at, 1), :] = cold[pl.ds(ask_ref[source, at] + 7, 1), :]
        for at in range(hot_cap):
            stage[pl.ds(first + cap + at, 1), :] = hot[pl.ds(ask_ref[source, hot_at + at] + 7, 1), :]
        return unused

    lax.fori_loop(0, shards, step, 0)
    narrow(stage, out_ref)


def pool_kernel(slot_ref, first_ref, bag_ref, back_ref, base_ref, wide_rows, stage, pooled, *, features):
    blocks = slot_ref.shape[0]
    window = LANES + 8
    widen(back_ref, wide_rows)
    pooled[...] = jnp.zeros_like(pooled)
    places = lax.broadcasted_iota(jnp.int32, (window, LANES), 0)

    def step(block, unused):
        for at in range(LANES):
            stage[at : at + 1, :] = wide_rows[pl.ds(slot_ref[block, at], 1), :]
        start = pl.multiple_of(first_ref[block, 0] // 8 * 8, 8)
        member = jnp.where(places + start == bag_ref[pl.ds(block, 1), :], 1.0, 0.0).astype(BF)
        part = jnp.dot(member, stage[...].astype(BF), preferred_element_type=F32)
        pooled[pl.ds(start, window), :] += part
        return unused

    lax.fori_loop(0, blocks, step, 0)
    samples = base_ref.shape[0]
    for feature in range(features):
        base_ref[:, feature * LANES : (feature + 1) * LANES] = pooled[
            pl.ds(feature, samples, stride=features), :
        ].astype(BF)


def spread_kernel(bag_ref, grad_ref, out_ref, bag_rows, stage, *, cap, hot_cap, hot_at, features):
    shards = bag_ref.shape[0]
    per_dest = cap + hot_cap
    samples = grad_ref.shape[0]
    for feature in range(features):
        bag_rows[pl.ds(feature, samples, stride=features), :] = grad_ref[
            :, feature * LANES : (feature + 1) * LANES
        ].astype(F32)

    def step(dest, unused):
        first = pl.multiple_of(dest * per_dest, 8)
        for at in range(per_dest):
            place = at if at < cap else hot_at + at - cap
            stage[pl.ds(first + at, 1), :] = bag_rows[pl.ds(bag_ref[dest, place], 1), :]
        return unused

    lax.fori_loop(0, shards, step, 0)
    narrow(stage, out_ref)


def hot_sum_kernel(ask_ref, in_ref, out_ref, wide_rows, stage, acc, *, cap, hot_cap):
    blocks, span = ask_ref.shape
    per_dest = cap + hot_cap
    group = span // hot_cap
    rows = acc.shape[0]
    row_ids = lax.broadcasted_iota(jnp.int32, (rows, span), 0) + 1
    widen(in_ref, wide_rows)
    acc[...] = jnp.zeros_like(acc)

    def step(block, unused):
        for member in range(group):
            first = pl.multiple_of((block * group + member) * per_dest + cap, 8)
            stage[member * hot_cap : (member + 1) * hot_cap, :] = wide_rows[pl.ds(first, hot_cap), :]
        pick = jnp.where(row_ids == ask_ref[pl.ds(block, 1), :], 1.0, 0.0).astype(BF)
        acc[...] += jnp.dot(pick, stage[...].astype(BF), preferred_element_type=F32)
        return unused

    lax.fori_loop(0, blocks, step, 0)
    out_ref[...] = acc[...].astype(out_ref.dtype)


def cold_sum_kernel(ask_ref, in_ref, out_ref, wide_rows, *, cap, hot_cap, hot_at):
    shards = ask_ref.shape[0]
    per_dest = cap + hot_cap
    rows = out_ref.shape[0]
    total = in_ref.shape[0]
    row_ids = lax.broadcasted_iota(jnp.int32, (rows, hot_at), 0) + 1
    widen(in_ref, wide_rows)
    wide_rows[total:, :] = jnp.zeros((wide_rows.shape[0] - total, LANES), F32)
    out_ref[...] = jnp.zeros_like(out_ref)

    def step(source, unused):
        first = pl.multiple_of(source * per_dest, 8)
        pick = jnp.where(row_ids == ask_ref[pl.ds(source, 1), :][:, :hot_at], 1.0, 0.0).astype(BF)
        block = wide_rows[pl.ds(first, hot_at), :].astype(BF)
        out_ref[...] += jnp.dot(pick, block, preferred_element_type=F32)
        return unused

    lax.fori_loop(0, shards, step, 0)


def shaped(shape, dtype):
    return jax.ShapeDtypeStruct(shape, dtype)


SMEM = pl.BlockSpec(memory_space=pltpu.SMEM)
VMEM = pl.BlockSpec(memory_space=pltpu.VMEM)


def body(
    hot_table,
    cold_table,
    bag_of,
    owner,
    row_in,
    cross_down,
    cross_up,
    cross_bias,
    top_weight,
    d_hidden,
    interpret=False,
):
    n_rep = lax.axis_size("rep")
    n_line = lax.axis_size("line")
    n_wide = n_line * CORES
    shards = n_rep * n_wide
    dests = n_wide + shards
    look_dev = row_in.shape[0]
    rows_dev = hot_table.shape[0]
    width = hot_table.shape[1]
    batch_dev = d_hidden.shape[0]
    feat_width = cross_down.shape[0]
    rank_width = cross_down.shape[1]
    features = feat_width // width
    bags_dev = batch_dev * features
    cap = max(8, (3 * look_dev // (2 * dests) + 7) // 8 * 8)
    hot_cap = round_up(-(-cap // n_rep), 8)
    per_dest = cap + hot_cap
    hot_at = round_up(cap, LANES)
    lanes = hot_at + round_up(hot_cap, LANES)
    total = shards * per_dest
    blocks = look_dev // LANES
    everyone = ("rep", "line", "core")
    plane = ("rep", "core")

    owner_2d = owner.reshape(blocks, LANES)
    bag_2d = bag_of.reshape(blocks, LANES)
    slots, ask, bag_pick = pl.pallas_call(
        functools.partial(
            route_kernel, n_rep=n_rep, n_wide=n_wide, cap=cap, per_dest=per_dest, hot_at=hot_at
        ),
        out_shape=(
            shaped((blocks, LANES), jnp.int32),
            shaped((shards, lanes), jnp.int32),
            shaped((shards, lanes), jnp.int32),
        ),
        in_specs=[VMEM] * 3,
        out_specs=(VMEM,) * 3,
        scratch_shapes=[
            pltpu.VMEM((round_up(dests, 16), LANES), F32),
            pltpu.VMEM((4 * shards, lanes), F32),
        ],
        interpret=interpret,
        name="route",
    )(owner_2d, row_in.reshape(blocks, LANES), bag_2d)
    asked = lax.all_to_all(ask, everyone, split_axis=0, concat_axis=0, tiled=True)
    found = pl.pallas_call(
        functools.partial(serve_kernel, cap=cap, hot_cap=hot_cap, hot_at=hot_at),
        out_shape=shaped((total, width), BF),
        in_specs=[SMEM, VMEM, VMEM],
        out_specs=VMEM,
        scratch_shapes=[
            pltpu.VMEM((rows_dev + 8, width), F32),
            pltpu.VMEM((rows_dev + 8, width), F32),
            pltpu.VMEM((total, width), F32),
        ],
        interpret=interpret,
        name="serve",
    )(asked, cold_table, hot_table)
    back = lax.all_to_all(found, everyone, split_axis=0, concat_axis=0, tiled=True)
    base = pl.pallas_call(
        functools.partial(pool_kernel, features=features),
        out_shape=shaped((batch_dev, feat_width), BF),
        in_specs=[SMEM, SMEM, VMEM, VMEM],
        out_specs=VMEM,
        scratch_shapes=[
            pltpu.VMEM((total, width), F32),
            pltpu.VMEM((LANES, width), F32),
            pltpu.VMEM((bags_dev + LANES + 8, width), F32),
        ],
        interpret=interpret,
        name="pool",
    )(slots, bag_2d, bag_2d, back)

    def by_plane(value):
        parts = value.reshape(batch_dev, n_rep, n_line, CORES, feat_width // shards)
        return parts.transpose(1, 3, 0, 2, 4).reshape(n_rep * CORES, batch_dev, -1)

    def to_all(value):
        return jnp.broadcast_to(value[None], (n_rep * CORES,) + value.shape)

    def exchange(pieces):
        joined = jnp.concatenate(pieces, axis=2)
        moved = lax.all_to_all(joined, plane, split_axis=0, concat_axis=0, tiled=True)
        return moved.reshape(n_rep * CORES * batch_dev, -1)

    part_width = n_line * (feat_width // shards)
    low = jnp.dot(base, cross_down, preferred_element_type=F32).astype(BF)
    cross = lax.dot_general(low, cross_up, NT, preferred_element_type=F32) + cross_bias
    base_full = base.astype(F32)
    mixed = (base_full * cross + base_full).astype(BF)
    early = exchange([by_plane(base), by_plane(mixed), to_all(low)])
    preact = jnp.dot(mixed, top_weight, preferred_element_type=F32)
    sigm = jax.nn.sigmoid(preact)
    d_pre = (d_hidden.astype(F32) * sigm * (1.0 + preact * (1.0 - sigm))).astype(BF)
    d_mixed = lax.dot_general(d_pre, top_weight, NT, preferred_element_type=F32)
    d_cross = (d_mixed * base_full).astype(BF)
    d_low = jnp.dot(d_cross, cross_up, preferred_element_type=F32).astype(BF)
    d_base = (
        d_mixed * (cross + 1.0) + lax.dot_general(d_low, cross_down, NT, preferred_element_type=F32)
    ).astype(BF)
    outgoing = pl.pallas_call(
        functools.partial(
            spread_kernel, cap=cap, hot_cap=hot_cap, hot_at=hot_at, features=features
        ),
        out_shape=shaped((total, width), BF),
        in_specs=[SMEM, VMEM],
        out_specs=VMEM,
        scratch_shapes=[
            pltpu.VMEM((bags_dev, width), F32),
            pltpu.VMEM((total, width), F32),
        ],
        interpret=interpret,
        name="spread",
    )(bag_pick, d_base)
    incoming = lax.all_to_all(outgoing, everyone, split_axis=0, concat_axis=0, tiled=True)
    late = exchange([by_plane(d_cross), to_all(d_low), to_all(d_pre)])

    contract = (((0,), (0,)), ((), ()))
    all_base = early[:, :part_width]
    all_mixed = early[:, part_width : 2 * part_width]
    all_low = early[:, 2 * part_width :]
    all_cross = late[:, :part_width]
    all_d_low = late[:, part_width : part_width + rank_width]
    all_pre = late[:, part_width + rank_width :]
    t_up = lax.dot_general(all_cross, all_low, contract, preferred_element_type=F32)
    t_down = lax.dot_general(all_base, all_d_low, contract, preferred_element_type=F32)
    t_top = lax.dot_general(all_mixed, all_pre, contract, preferred_element_type=F32)
    part = jnp.concatenate([t_up, t_down, t_top], axis=1).astype(BF)
    part = lax.all_to_all(
        part.reshape(n_line, feat_width // shards, -1), "line", split_axis=0, concat_axis=0, tiled=True
    )
    scale_factor = 1.0 / math.sqrt(batch_dev * shards)
    summed = jnp.sum(part.astype(F32), axis=0) * scale_factor

    hot_span = math.gcd(shards * hot_cap, 256)
    hot_asked = asked[:, hot_at : hot_at + hot_cap].reshape(-1, hot_span)
    hot_part = pl.pallas_call(
        functools.partial(hot_sum_kernel, cap=cap, hot_cap=hot_cap),
        out_shape=shaped((rows_dev, width), BF),
        in_specs=[VMEM, VMEM],
        out_specs=VMEM,
        scratch_shapes=[
            pltpu.VMEM((total, width), F32),
            pltpu.VMEM((hot_span, width), F32),
            pltpu.VMEM((rows_dev, width), F32),
        ],
        interpret=interpret,
        name="hot_sum",
    )(hot_asked, incoming)
    hot_all = lax.all_to_all(
        jnp.broadcast_to(hot_part[None], (n_rep,) + hot_part.shape),
        "rep",
        split_axis=0,
        concat_axis=0,
        tiled=True,
    )
    hot_grad = jnp.sum(hot_all.astype(F32), axis=0)
    cold_grad = pl.pallas_call(
        functools.partial(cold_sum_kernel, cap=cap, hot_cap=hot_cap, hot_at=hot_at),
        out_shape=shaped((rows_dev, width), F32),
        in_specs=[VMEM, VMEM],
        out_specs=VMEM,
        scratch_shapes=[pltpu.VMEM((total + hot_at, width), F32)],
        interpret=interpret,
        name="cold_sum",
    )(asked, incoming)
    return (
        summed[:, :rank_width],
        summed[:, rank_width : 2 * rank_width],
        summed[:, 2 * rank_width :],
        hot_grad,
        cold_grad,
    )


def solution(mesh):
    n_rep, n_wide = mesh.devices.shape
    fine = Mesh(mesh.devices.reshape(n_rep, n_wide // CORES, CORES), ("rep", "line", "core"))
    every = ("rep", "line", "core")
    wide = ("line", "core")
    placed = (
        P(wide, None),
        P(every, None),
        P(every, None),
        P(every, None),
        P(every),
        P(),
        P(),
        P(),
        P(),
        P(every, None),
    )
    return jax.shard_map(
        body,
        mesh=fine,
        in_specs=placed,
        out_specs=(
            P(every, None),
            P(every, None),
            P(every, None),
            P(wide, None),
            P(every, None),
        ),
        check_vma=False,
    )
```

time: 709 us -> 348 us (0.49); the launches traced: 695 us -> 347 us
  other arithmetic: 262 us -> 8.91 us
  waiting for transfers between devices: 216 us -> 94.9 us
  Pallas kernels: 0 us -> 90.2 us
  blocking collectives: 0 us -> 74.9 us
  local copies, waits for them, and re-layouts: 106 us -> 36.8 us
  matrix products: 65.7 us -> 19.7 us
  between operations: 16 us -> 0.85 us
    reduce_sum x157 -> x2, other arithmetic: 232 us -> 3.14 us  [the longest x1 2.96 us: body(): hot_grad = jnp.sum(hot_all.astype(F32), axis=0)]
    pallas_call x0 -> x6, Pallas kernels: none -> 90.2 us  [the longest x1 18.2 us: body(): pl.pallas_call(functools.partial(pool_kernel, features=features), out_sha...]
    reduce_scatter x1 -> x0, waiting for transfers between devices: 75.8 us -> none  [body(): lax.psum_scatter(jnp.concatenate([t_up, t_down, t_top], axis=1) * scale_f...]
    all_to_all x0 -> x2, blocking collectives: none -> 74.9 us  [the longest x1 60.5 us: body(): lax.all_to_all(found, everyone, split_axis=0, concat_axis=0, tiled=True)]
    gather x4 -> x0, local copies, waits for them, and re-layouts: 63 us -> none  [the longest x1 23.1 us: body(): look_rows = returned[slots]]
    dot_general x22 -> x9, matrix products: 65.7 us -> 19.7 us  [the longest x1 4.65 us: body(): lax.dot_general(d_low, cross_down, NT, preferred_element_type=F32)]
    all_to_all x6 -> x5, waiting for transfers between devices: 140 us -> 94.9 us  [the longest x1 41 us: body(): lax.all_to_all(outgoing, everyone, split_axis=0, concat_axis=0, tiled=True)]
    dynamic_update_slice x447 -> x0, local copies, waits for them, and re-layouts: 16.8 us -> none  [the longest x435 16.1 us: blocked(): result = lax.map(fn, index_blocks)]
  transfers between devices with their start and end apart: 8 -> 5, of which waited for: 6 -> 5; matrix products, arithmetic and copies ran while one was open for 13% -> 11% of each run, Pallas kernels for 0% -> 11%
where the time goes in v1:
time: 348 us; the launch traced here: 347 us
  waiting for transfers between devices  94.9 us (27%)
  Pallas kernels  90.2 us (26%)
  blocking collectives  74.9 us (22%)
  local copies, waits for them, and re-layouts  36.8 us (11%)
  starting transfers between devices  20.5 us (6%)
  matrix products  19.7 us (6%)
  other arithmetic  8.91 us (3%)
    all_to_all x1, blocking collectives, body(): lax.all_to_all(found, everyone, split_axis=0, concat_axis=0, tiled=True)  60.5 us
    all_to_all x1, waiting for transfers between devices, body(): lax.all_to_all(outgoing, everyone, split_axis=0, concat_axis=0, tiled=True)  41 us
    all_to_all x2, waiting for transfers between devices, exchange(): lax.all_to_all(joined, plane, split_axis=0, concat_axis=0, tiled=True)  30.5 us
    pallas_call x1, Pallas kernels, body(): pl.pallas_call(functools.partial(pool_kernel, features=features), out_sha...  18.2 us
    pallas_call x1, Pallas kernels, body(): pl.pallas_call(functools.partial(route_kernel, n_rep=n_rep, n_wide=n_wide...  18.2 us
    all_to_all x1, waiting for transfers between devices, body(): lax.all_to_all(part.reshape(n_line, feat_width // shards, -1), 'line', sp...  17.8 us
    pallas_call x1, Pallas kernels, body(): pl.pallas_call(functools.partial(cold_sum_kernel, cap=cap, hot_cap=hot_ca...  17.3 us
    reshape x6, local copies, waits for them, and re-layouts, by_plane(): parts = value.reshape(batch_dev, n_rep, n_line, CORES, feat_width // shards)  16.6 us
  transfers between devices with their start and end apart: 5, of which 5 were waited for; matrix products, arithmetic and copies ran while one was open for 11% of the time, Pallas kernels for 11%

profile of v1, /device:TPU:0, one launch (start us, length us, event | category | flops | bytes accessed | tf_op | source)
XLA Modules:
  0.0 346.7 jit_solution(12928583242633902418)
XLA Ops:
  0.6 18.2 %route.1 = (s32[48,128]{1,0:T(8,128)}, s32[32,384]{1,0:T(8,128)}, s32[32,384]{1,0:T(8,128)}) custom-call(s32[48,128]{1,0:T(8,128)} %bitcast.58, s32[48,128]{1,0:T(8,128)} %bitcast.59, s32[48,128]{1,0:T(8,128)} %bitcast.54), custom_call_target="tpu_custom_call" | custom-call | tf_op jit(solution)/shard_map/route/pallas_call | solution.py:243
  18.8 0.8 copy.38
  19.7 14.5 %all_to_all.53 = s32[32,1,384]{2,1,0:T(1,128)S(1)} all-to-all(s32[32,1,384]{2,1,0:T(1,128)S(1)} %copy.38), channel_id=1, replica_groups=mesh['rep'=4,'line'=4,'core'=2] {'rep','line','core'}, dimensions={0} | all-to-all | bytes 98304 | tf_op jit(solution)/shard_map/all_to_all | solution.py:261
  34.8 13.9 %serve.1 = bf16[9472,128]{1,0:T(8,128)(2,1)} custom-call(s32[32,384]{1,0:T(8,128)} %bitcast.48, bf16[2048,128]{1,0:T(8,128)(2,1)} %cold_ref.1, bf16[2048,128]{1,0:T(8,128)(2,1)} %hot_ref.1), custom_call_target="tpu_custom_call" | custom-call | tf_op jit(solution)/shard_map/serve/pallas_call | solution.py:262
  48.7 60.5 %all_to_all.54 = bf16[32,296,128]{2,1,0:T(8,128)(2,1)} all-to-all(bf16[32,296,128]{2,1,0:T(8,128)(2,1)} %bitcast.38), channel_id=1, replica_groups=mesh['rep'=4,'line'=4,'core'=2] {'rep','line','core'}, dimensions={0} | all-to-all | bytes 4849664 | tf_op jit(solution)/shard_map/all_to_all | solution.py:275
  109.1 18.2 %pool.1 = bf16[128,4096]{1,0:T(8,128)(2,1)} custom-call(s32[48,128]{1,0:T(8,128)} %get-tuple-element.8.slot_ref, s32[48,128]{1,0:T(8,128)} %bitcast.55, s32[48,128]{1,0:T(8,128)} %bitcast.56, bf16[9472,128]{1,0:T(8,128)(2,1)} %bitcast.37), custom_call_target="tpu_custom_call" | custom-call | tf_op jit(solution)/shard_map/pool/pallas_call | solution.py:276
  127.4 2.4 convolution_convert_fusion.4
  129.9 2.2 fusion.2
  132.1 0.7 copy-done.5
  132.8 1.5 multiply_convert_fusion
  134.3 2.8 fusion.1
  137.1 1.0 copy-done.2
  138.5 2.6 reshape.67
  141.2 3.7 %copy.39 = bf16[128,4,4,2,128]{0,4,2,3,1:T(8,128)(2,1)} copy(bf16[128,4,4,2,128]{4,3,2,1,0:T(2,128)(2,1)} %reshape.67) | data formatting | bytes 2097152 | tf_op jit(solution)/shard_map/reshape | solution.py:291
  144.8 1.0 copy.41
  146.1 1.0 copy-done.4
  147.1 1.7 pad_maximum_fusion
  148.8 4.4 %all-to-all-start.2 = ((bf16[8,128,1280]{1,2,0:T(8,128)(2,1)}), bf16[8,128,1280]{1,2,0:T(8,128)(2,1)}, u32[]{:S(2)}, u32[]{:S(2)}) async-start(bf16[8,128,1280]{1,2,0:T(8,128)(2,1)} %pad_maximum_fusion), calls=%async_computation.2 | async-start | bytes 5242880 | tf_op jit(solution)/shard_map/all_to_all | solution.py:299
  153.2 2.6 reshape.72
  155.9 1.6 reshape.70
  157.4 2.6 copy.44
  160.0 3.7 %copy.43 = bf16[128,4,4,2,128]{0,4,2,3,1:T(8,128)(2,1)} copy(bf16[128,4,4,2,128]{4,3,2,1,0:T(2,128)(2,1)} %reshape.70) | data formatting | bytes 2097152 | tf_op jit(solution)/shard_map/reshape | solution.py:291
  163.8 2.9 pad_maximum_fusion.1
  166.7 18.8 %all-to-all-done.2 = bf16[8,128,1280]{1,2,0:T(8,128)(2,1)} async-done(((bf16[8,128,1280]{1,2,0:T(8,128)(2,1)}), bf16[8,128,1280]{1,2,0:T(8,128)(2,1)}, u32[]{:S(2)}, u32[]{:S(2)}) %all-to-all-start.2) | async-done | bytes 2621472 | tf_op jit(solution)/shard_map/all_to_all | solution.py:299
  185.5 4.4 %all-to-all-start.3 = ((bf16[8,128,1280]{1,2,0:T(8,128)(2,1)}), bf16[8,128,1280]{1,2,0:T(8,128)(2,1)}, u32[]{:S(2)}, u32[]{:S(2)}) async-start(bf16[8,128,1280]{1,2,0:T(8,128)(2,1)} %pad_maximum_fusion.1), calls=%async_computation.3 | async-start | bytes 5242880 | tf_op jit(solution)/shard_map/all_to_all | solution.py:299
  189.9 4.7 %fusion.grad_ref = bf16[128,4096]{1,0:T(8,128)(2,1)} fusion(bf16[128,256]{1,0:T(8,128)(2,1)S(1)} %convolution_convert_fusion.3, bf16[4096,256]{1,0:T(8,128)(2,1)} %param.15, f32[128,4096]{1,0:T(8,128)} %get-tuple-element.18, f32[128,4096]{1,0:T(8,128)} %get-tuple-element.14), kind=kOutput, calls=%fused_computation.2 | convolution fusion | flops 270532608 | bytes 7405568 | tf_op jit(solution)/shard_map/dot_general | solution.py:315
  194.5 15.9 %spread.1 = bf16[9472,128]{1,0:T(8,128)(2,1)} custom-call(s32[32,384]{1,0:T(8,128)} %get-tuple-element.10.bag_ref, bf16[128,4096]{1,0:T(8,128)(2,1)} %fusion.grad_ref), custom_call_target="tpu_custom_call" | custom-call | tf_op jit(solution)/shard_map/spread/pallas_call | solution.py:317
  210.4 11.7 %all-to-all-done.3 = bf16[8,128,1280]{1,2,0:T(8,128)(2,1)} async-done(((bf16[8,128,1280]{1,2,0:T(8,128)(2,1)}), bf16[8,128,1280]{1,2,0:T(8,128)(2,1)}, u32[]{:S(2)}, u32[]{:S(2)}) %all-to-all-start.3) | async-done | bytes 2621472 | tf_op jit(solution)/shard_map/all_to_all | solution.py:299
  222.1 3.7 %all-to-all-start.5 = ((bf16[32,296,128]{2,1,0:T(8,128)(2,1)}), bf16[32,296,128]{2,1,0:T(8,128)(2,1)}, u32[]{:S(2)}, u32[]{:S(2)}) async-start(bf16[32,296,128]{2,1,0:T(8,128)(2,1)} %bitcast.36), calls=%async_computation.5 | async-start | bytes 4849664 | tf_op jit(solution)/shard_map/all_to_all | solution.py:331
  225.8 4.4 %copy.42 = bf16[8,128,1280]{2,1,0:T(8,128)(2,1)} copy(bf16[8,128,1280]{1,2,0:T(8,128)(2,1)} %all-to-all-done.2) | data formatting | bytes 5242880 | tf_op jit(solution)/shard_map/all_to_all | solution.py:299
  230.2 4.4 %copy.46 = bf16[8,128,1280]{2,1,0:T(8,128)(2,1)} copy(bf16[8,128,1280]{1,2,0:T(8,128)(2,1)} %all-to-all-done.3) | data formatting | bytes 5242880 | tf_op jit(solution)/shard_map/all_to_all | solution.py:299
  234.6 2.0 convolution_convert_fusion.2
  236.9 1.7 convolution_convert_fusion.1
  238.6 2.0 convolution_convert_fusion
  240.5 1.1 pad_maximum_fusion.2
  241.7 41.0 %all-to-all-done.5 = bf16[32,296,128]{2,1,0:T(8,128)(2,1)} async-done(((bf16[32,296,128]{2,1,0:T(8,128)(2,1)}), bf16[32,296,128]{2,1,0:T(8,128)(2,1)}, u32[]{:S(2)}, u32[]{:S(2)}) %all-to-all-start.5) | async-done | bytes 2424864 | tf_op jit(solution)/shard_map/all_to_all | solution.py:331
  282.6 3.5 %all-to-all-start.4 = ((bf16[4,128,1024]{2,1,0:T(8,128)(2,1)}), bf16[4,128,1024]{2,1,0:T(8,128)(2,1)S(1)}, u32[]{:S(2)}, u32[]{:S(2)}) async-start(bf16[4,128,1024]{2,1,0:T(8,128)(2,1)} %pad_maximum_fusion.2), calls=%async_computation.4 | async-start | bytes 2097152 | tf_op jit(solution)/shard_map/all_to_all | solution.py:345
  286.2 0.7 slice.49
  286.9 0.7 reshape.75.ask_ref
  287.6 6.7 %hot_sum.1 = bf16[2048,128]{1,0:T(8,128)(2,1)} custom-call(s32[8,256]{1,0:T(8,128)} %reshape.75.ask_ref, bf16[9472,128]{1,0:T(8,128)(2,1)} %bitcast.18.in_ref), custom_call_target="tpu_custom_call" | custom-call | tf_op jit(solution)/shard_map/hot_sum/pallas_call | solution.py:353
  294.2 17.8 %all-to-all-done.4 = bf16[4,128,1024]{2,1,0:T(8,128)(2,1)S(1)} async-done(((bf16[4,128,1024]{2,1,0:T(8,128)(2,1)}), bf16[4,128,1024]{2,1,0:T(8,128)(2,1)S(1)}, u32[]{:S(2)}, u32[]{:S(2)}) %all-to-all-start.4) | async-done | bytes 1048608 | tf_op jit(solution)/shard_map/all_to_all | solution.py:345
  312.1 2.6 broadcast_in_dim.11
  314.7 4.5 %all-to-all-start.6 = ((bf16[4,2048,128]{2,1,0:T(8,128)(2,1)}), bf16[4,2048,128]{2,1,0:T(8,128)(2,1)}, u32[]{:S(2)}, u32[]{:S(2)}) async-start(bf16[4,2048,128]{2,1,0:T(8,128)(2,1)} %broadcast_in_dim.11), calls=%async_computation.6 | async-start | bytes 4194304 | tf_op jit(solution)/shard_map/all_to_all | solution.py:366
  319.4 0.7 slice.48
  320.1 0.7 fusion.13
  320.8 17.3 %cold_sum.1 = f32[2048,128]{1,0:T(8,128)} custom-call(s32[32,384]{1,0:T(8,128)} %bitcast.50, bf16[9472,128]{1,0:T(8,128)(2,1)} %bitcast.18.in_ref), custom_call_target="tpu_custom_call" | custom-call | tf_op jit(solution)/shard_map/cold_sum/pallas_call | solution.py:374
  338.2 5.6 %all-to-all-done.6 = bf16[4,2048,128]{2,1,0:T(8,128)(2,1)} async-done(((bf16[4,2048,128]{2,1,0:T(8,128)(2,1)}), bf16[4,2048,128]{2,1,0:T(8,128)(2,1)}, u32[]{:S(2)}, u32[]{:S(2)}) %all-to-all-start.6) | async-done | bytes 2097184 | tf_op jit(solution)/shard_map/all_to_all | solution.py:366
  343.7 3.0 convert_reduce_fusion
  (24 shorter events, 2.0 us)
Async XLA Ops:
  0.6 129.2 %copy-start = (bf16[4096,256]{1,0:T(8,128)(2,1)S(1)}, bf16[4096,256]{1,0:T(8,128)(2,1)}, u32[]{:S(2)}) copy-start(bf16[4096,256]{1,0:T(8,128)(2,1)} %param.16) | copy-start | bytes 6291460
  127.4 2.5 copy-start.1
  127.4 2.5 copy-start.8
  129.8 2.9 copy-start.5
  129.9 2.9 copy-start.7
  132.1 2.2 copy-start.3
  137.1 1.0 copy-start.2
  145.9 1.2 copy-start.4
  148.8 36.6 %all-to-all-start.2 = ((bf16[8,128,1280]{1,2,0:T(8,128)(2,1)}), bf16[8,128,1280]{1,2,0:T(8,128)(2,1)}, u32[]{:S(2)}, u32[]{:S(2)}) async-start(bf16[8,128,1280]{1,2,0:T(8,128)(2,1)} %pad_maximum_fusion), calls=%async_computation.2 | async-start | bytes 5242880 | tf_op jit(solution)/shard_map/all_to_all | solution.py:299
  185.5 36.7 %all-to-all-start.3 = ((bf16[8,128,1280]{1,2,0:T(8,128)(2,1)}), bf16[8,128,1280]{1,2,0:T(8,128)(2,1)}, u32[]{:S(2)}, u32[]{:S(2)}) async-start(bf16[8,128,1280]{1,2,0:T(8,128)(2,1)} %pad_maximum_fusion.1), calls=%async_computation.3 | async-start | bytes 5242880 | tf_op jit(solution)/shard_map/all_to_all | solution.py:299
  222.1 60.5 %all-to-all-start.5 = ((bf16[32,296,128]{2,1,0:T(8,128)(2,1)}), bf16[32,296,128]{2,1,0:T(8,128)(2,1)}, u32[]{:S(2)}, u32[]{:S(2)}) async-start(bf16[32,296,128]{2,1,0:T(8,128)(2,1)} %bitcast.36), calls=%async_computation.5 | async-start | bytes 4849664 | tf_op jit(solution)/shard_map/all_to_all | solution.py:331
  234.6 2.2 copy-start.6
  282.6 29.4 %all-to-all-start.4 = ((bf16[4,128,1024]{2,1,0:T(8,128)(2,1)}), bf16[4,128,1024]{2,1,0:T(8,128)(2,1)S(1)}, u32[]{:S(2)}, u32[]{:S(2)}) async-start(bf16[4,128,1024]{2,1,0:T(8,128)(2,1)} %pad_maximum_fusion.2), calls=%async_computation.4 | async-start | bytes 2097152 | tf_op jit(solution)/shard_map/all_to_all | solution.py:345
  314.7 29.0 %all-to-all-start.6 = ((bf16[4,2048,128]{2,1,0:T(8,128)(2,1)}), bf16[4,2048,128]{2,1,0:T(8,128)(2,1)}, u32[]{:S(2)}, u32[]{:S(2)}) async-start(bf16[4,2048,128]{2,1,0:T(8,128)(2,1)} %broadcast_in_dim.11), calls=%async_computation.6 | async-start | bytes 4194304 | tf_op jit(solution)/shard_map/all_to_all | solution.py:366
